TPU v7x, 32 devices: a whole 2x2x4 slice. The times are simulated.
32 devices in a mesh: rows: 16 (over z, y, x), cols: 2 (over core).
Axes of the slice: x: 2, y: 2, z: 4, core: 2. Of those that a mesh axis runs over, the one named last changes fastest.
Arguments:
- points: float32 [8, 4096], P(None, ('cols', 'rows')), may hold values from -6 to 6
- targets: float32 [4096], P(('cols', 'rows')), may hold values from -6 to 6
- noise: float32 [64, 4096], P(None, ('cols', 'rows')), may hold values from -6 to 6
- omega: float32 [8, 2048], P(None, 'rows'), may hold values from -12 to 12
- phase: float32 [2048], P('rows'), may hold values from -3.140625 to 3.140625
- weights: float32 [2048, 64], P('rows'), may hold values from -6 to 6
Outputs:
- posterior: float32 [64, 4096], P(None, ('cols', 'rows'))
- residual: float32 [64, 4096], P(None, ('cols', 'rows'))
All inputs are finite; a program needn't handle non-finite values.
Results may differ from a plain program's by a relative error of at most 0.02.
Values may be sent and summed in bfloat16 or wider, within the bound.
A program may use at most 64 MiB of HBM per device.

v0:
```python
import math

import jax
import jax.numpy as jnp
from jax import lax
from jax.sharding import PartitionSpec as P

ITERS = 2


def kernel_block(left, right):
    cross = lax.dot_general(
        left,
        right,
        (((0,), (0,)), ((), ())),
        precision=lax.Precision.HIGHEST,
        preferred_element_type=jnp.float32,
    )
    left_sq = jnp.sum(left * left, 0)
    right_sq = jnp.sum(right * right, 0)
    dist = left_sq[:, None] + right_sq[None, :] - 2.0 * cross
    return jnp.exp(-2.0 * dist).astype(jnp.bfloat16)


def body(points, targets, noise, omega, phase, weights):
    wide_omega, wide_phase, wide_weights = (
        lax.all_gather(omega, "rows", axis=1, tiled=True),
        lax.all_gather(phase, "rows", axis=0, tiled=True),
        lax.all_gather(weights, "rows", axis=0, tiled=True),
    )
    features = jnp.cos(
        lax.dot_general(
            wide_omega,
            points,
            (((0,), (0,)), ((), ())),
            precision=lax.Precision.HIGHEST,
            preferred_element_type=jnp.float32,
        )
        + wide_phase[:, None]
    )
    prior = math.sqrt(2.0 / wide_weights.shape[0]) * lax.dot_general(
        wide_weights,
        features,
        (((0,), (0,)), ((), ())),
        precision=lax.Precision.HIGHEST,
        preferred_element_type=jnp.float32,
    )
    rhs = targets[None, :] - prior - 0.5 * noise
    columns = lax.all_gather(points, ("rows", "cols"), axis=1, tiled=True)
    residual = rhs
    direction = rhs
    posterior = prior
    norm_now = lax.psum(jnp.sum(residual * residual, 1), ("rows", "cols"))
    for step in range(ITERS):
        low = direction.astype(jnp.bfloat16)
        kernel_part = jnp.dot(
            lax.all_gather(low, ("rows", "cols"), axis=1, tiled=True),
            kernel_block(columns, points),
            preferred_element_type=jnp.float32,
        )
        image = kernel_part + 0.25 * direction
        curve, mixed, square = lax.psum(
            (
                jnp.sum(direction * image, 1),
                jnp.sum(residual * image, 1),
                jnp.sum(image * image, 1),
            ),
            ("rows", "cols"),
        )
        alpha = norm_now / curve
        norm_next = norm_now - 2.0 * alpha * mixed + alpha * alpha * square
        posterior = posterior + alpha[:, None] * kernel_part
        residual = residual - alpha[:, None] * image
        if step + 1 < ITERS:
            direction = residual + (norm_next / norm_now)[:, None] * direction
            norm_now = norm_next
    return (posterior, residual)


def solution(mesh):
    return jax.shard_map(
        body,
        mesh=mesh,
        in_specs=(
            P(None, ("cols", "rows")),
            P(("cols", "rows")),
            P(None, ("cols", "rows")),
            P(None, "rows"),
            P("rows"),
            P("rows", None),
        ),
        out_specs=(P(None, ("cols", "rows")), P(None, ("cols", "rows"))),
        check_vma=False,
    )
```

profile of v0, /device:TPU:0, one launch (start us, length us, event | category | flops | bytes accessed | tf_op | source)
XLA Modules:
  0.0 325.3 jit_solution(18356954355384367689)
XLA Ops:
  0.6 0.0 copy-start.1
  0.6 0.0 copy-start.3
  0.7 0.0 copy-start.2
  0.7 43.1 %all_gather.18 = f32[8,2048]{1,0:T(8,128)S(1)} all-gather(f32[8,128]{1,0:T(8,128)} %param.9), channel_id=1, replica_groups=mesh['rows'=16,'cols'=2] {'rows'}, dimensions={1}, use_global_device_ids=true | all-gather | bytes 69632 | tf_op jit(solution)/shard_map/all_gather | solution.py:27
  43.8 35.7 %all-gather = f32[16,1,128]{2,1,0:T(1,128)S(1)} all-gather(f32[1,1,128]{2,1,0:T(1,128)} %bitcast.15), channel_id=1, replica_groups=mesh['rows'=16,'cols'=2] {'rows'}, dimensions={0}, use_global_device_ids=true | all-gather | bytes 8704 | tf_op jit(solution)/shard_map/all_gather | solution.py:28
  79.5 7.0 %fusion.4 = f32[2048,128]{1,0:T(8,128)S(1)} fusion(f32[8,2048]{1,0:T(8,128)S(1)} %all_gather.18, f32[8,128]{1,0:T(8,128)} %param.6, f32[2048]{0:T(1024)S(1)} %bitcast.14), kind=kOutput, calls=%fused_computation.6 | convolution fusion | flops 25427968 | bytes 1126400 | tf_op jit(solution)/shard_map/dot_general | solution.py:32
  86.5 0.0 copy-done.1
  86.5 0.0 copy-start
  86.5 40.4 %all_gather.20 = f32[2048,64]{0,1:T(8,128)S(1)} all-gather(f32[128,64]{0,1:T(8,128)S(1)} %copy-done.1), channel_id=1, replica_groups=mesh['rows'=16,'cols'=2] {'rows'}, dimensions={0}, use_global_device_ids=true | all-gather | bytes 557056 | tf_op jit(solution)/shard_map/all_gather | solution.py:29
  127.0 0.0 copy-done.3
  127.0 0.0 copy-done.2
  127.0 0.8 fusion.8
  127.8 0.0 copy-done
  127.8 36.8 %all_gather.22 = f32[8,4096]{1,0:T(8,128)S(1)} all-gather(f32[8,128]{1,0:T(8,128)S(1)} %copy-done), channel_id=1, replica_groups=mesh['rows'=16,'cols'=2] {'rows','cols'}, dimensions={1}, use_global_device_ids=true | all-gather | bytes 135168 | tf_op jit(solution)/shard_map/all_gather | solution.py:49
  164.6 3.9 %fusion.3 = bf16[4096,128]{1,0:T(8,128)(2,1)S(1)} fusion(f32[8,4096]{1,0:T(8,128)S(1)} %all_gather.22, f32[8,128]{1,0:T(8,128)S(1)} %copy-done, f32[128]{0:T(128)S(1)} %multiply_reduce_fusion.5, f32[4096]{0:T(1024)S(1)} %multiply_reduce_fusion), kind=kOutput, calls=%fused_computation.4 | convolution fusion | flops 52953088 | bytes 1200640 | tf_op jit(solution)/shard_map/dot_general | solution.py:12
  168.5 39.8 %all_gather.21 = bf16[64,4096]{1,0:T(8,128)(2,1)S(1)} all-gather(bf16[64,128]{1,0:T(8,128)(2,1)S(1)} %get-tuple-element.11), channel_id=1, replica_groups=mesh['rows'=16,'cols'=2] {'rows','cols'}, dimensions={1}, use_global_device_ids=true | all-gather | bytes 540672 | tf_op jit(solution)/shard_map/all_gather | solution.py:57
  208.3 0.4 multiply_reduce_fusion.3
  208.8 36.9 %all-reduce = (f32[64]{0:T(128)S(1)}, f32[64]{0:T(128)S(1)}, f32[64]{0:T(128)S(1)}) all-reduce(f32[64]{0:T(128)S(1)} %get-tuple-element.3, f32[64]{0:T(128)S(1)} %get-tuple-element.4, f32[64]{0:T(128)S(1)} %get-tuple-element.2), channel_id=1, replica_groups=mesh['rows'=16,'cols'=2] {'rows','cols'}, use_global_device_ids=true, to_apply=%region_7.0 | all-reduce | flops 192 | bytes 1536 | tf_op jit(solution)/shard_map/psum | solution.py:62
  245.6 0.1 fusion.6
  245.7 41.6 %all_gather.23 = bf16[64,4096]{1,0:T(8,128)(2,1)S(1)} all-gather(bf16[64,128]{1,0:T(8,128)(2,1)S(1)} %fusion.6), channel_id=1, replica_groups=mesh['rows'=16,'cols'=2] {'rows','cols'}, dimensions={1}, use_global_device_ids=true | all-gather | bytes 540672 | tf_op jit(solution)/shard_map/all_gather | solution.py:57
  287.3 0.4 multiply_reduce_fusion.1
  287.7 36.8 %psum.34 = f32[64]{0:T(128)S(1)} all-reduce(f32[64]{0:T(128)S(1)} %get-tuple-element.17), channel_id=1, replica_groups=mesh['rows'=16,'cols'=2] {'rows','cols'}, use_global_device_ids=true, to_apply=%region_9.0 | all-reduce | flops 64 | bytes 512 | tf_op jit(solution)/shard_map/psum | solution.py:62
  324.6 0.7 multiply_subtract_fusion
  (4 shorter events, 0.1 us)
Async XLA Ops:
  0.6 85.9 %copy-start.1 = (f32[128,64]{0,1:T(8,128)S(1)}, f32[128,64]{0,1:T(8,128)}, u32[]{:S(2)}) copy-start(f32[128,64]{0,1:T(8,128)} %param.11) | copy-start | bytes 98308
  0.6 126.3 %copy-start.3 = (f32[128]{0:T(128)S(1)}, f32[128]{0:T(128)}, u32[]{:S(2)}) copy-start(f32[128]{0:T(128)} %param.7) | copy-start | bytes 1540
  0.7 126.3 %copy-start.2 = (f32[64,128]{1,0:T(8,128)S(1)}, f32[64,128]{1,0:T(8,128)}, u32[]{:S(2)}) copy-start(f32[64,128]{1,0:T(8,128)} %param.8) | copy-start | bytes 98308
  86.5 41.2 %copy-start = (f32[8,128]{1,0:T(8,128)S(1)}, f32[8,128]{1,0:T(8,128)}, u32[]{:S(2)}) copy-start(f32[8,128]{1,0:T(8,128)} %param.6) | copy-start | bytes 12292
where the time goes:
time: 326 us; the launch traced here: 325 us
  blocking collectives  311 us (95%)
  matrix products  12.5 us (4%)
    all_gather x2, blocking collectives, body(): lax.all_gather(low, ('rows', 'cols'), axis=1, tiled=True)  81.4 us
    psum x2, blocking collectives, body(): lax.psum((jnp.sum(direction * image, 1), jnp.sum(residual * image, 1), jn...  73.7 us
    all_gather x1, blocking collectives, body(): lax.all_gather(omega, 'rows', axis=1, tiled=True)  43.1 us
    all_gather x1, blocking collectives, body(): lax.all_gather(weights, 'rows', axis=0, tiled=True)  40.4 us
    all_gather x1, blocking collectives, body(): columns = lax.all_gather(points, ('rows', 'cols'), axis=1, tiled=True)  36.8 us
    all_gather x1, blocking collectives, body(): lax.all_gather(phase, 'rows', axis=0, tiled=True)  35.7 us
    dot_general x1, matrix products, body(): lax.dot_general(wide_omega, points, (((0,), (0,)), ((), ())), precision=l...  7.01 us

commit v1 on v0

v1 whole, which is shorter than its diff:
```python
import functools
import math

import jax
import jax.numpy as jnp
from jax import lax
from jax.experimental import pallas as pl
from jax.experimental.pallas import tpu as pltpu
from jax.sharding import PartitionSpec as P

MESH = pl.DeviceIdType.MESH
LOG2E = math.log2(math.e)
COS = (
    0.9999999889,
    -19.73920447,
    64.93911593,
    -85.45011343,
    60.16742979,
    -25.96688461,
    6.527705963,
)
PTS, OMG, PHA, WTS, LOW, IMG, LOWF, IMGF, ST0, ST1, ST2 = range(11)
KINDS = 11


def loop(count, body):
    if count <= 32:
        for k in range(count):
            body(k)
    else:
        lax.fori_loop(0, count, lambda k, c: (body(k), c)[1], 0)


def split(x):
    high = x.astype(jnp.bfloat16).astype(jnp.float32)
    rest = x - high
    mid = rest.astype(jnp.bfloat16).astype(jnp.float32)
    return high, mid, rest - mid


def rows_of(x):
    high, mid, low = split(x)
    at = lax.broadcasted_iota(jnp.int32, (8, x.shape[1]), 0)
    return jnp.where(at == 0, high, jnp.where(at == 1, mid, jnp.where(at == 2, low, 0.0)))


def right_stack(x, seventh, eighth):
    high, mid, low = split(x)
    parts = (high, mid, low, high, mid, high, seventh, eighth)
    return jnp.concatenate(parts, 0).astype(jnp.bfloat16)


def cosine(turns):
    r = turns - jnp.floor(turns + 0.5)
    y = r * r
    out = COS[-1]
    for c in COS[-2::-1]:
        out = out * y + c
    return out


def nt(a, b):
    return lax.dot_general(a, b, (((1,), (1,)), ((), ())), preferred_element_type=jnp.float32)


def kernel(
    R, C, scale,
    points, targets, noise, omega, phase, weights,
    post_out, res_out,
    pts, omg, pha, wts, low, img, kern, st0, st1, st2, coef, ssem, rsem, slots,
):
    n = R * C
    me_r = lax.axis_index("rows")
    me_c = lax.axis_index("cols")
    me = me_c * R + me_r
    S = noise.shape[0]
    B = noise.shape[1]

    barrier = pltpu.get_barrier_semaphore()

    def other(k):
        j = lax.rem(me + k, n)
        return j, (lax.rem(j, R), j // R)

    def hello(k):
        pl.semaphore_signal(barrier, inc=1, device_id=other(k + 1)[1], device_id_type=MESH)

    loop(n - 1, hello)

    def send(buf, slot, kind, to):
        return pltpu.make_async_remote_copy(
            src_ref=buf.at[slot], dst_ref=buf.at[slot],
            send_sem=ssem.at[kind],
            recv_sem=slots.at[kind - LOW, lax.rem(slot, R)] if kind in (LOW, IMG) else rsem.at[kind],
            device_id=to, device_id_type=MESH,
        )

    def many(buf, count, kind):
        return pltpu.make_async_remote_copy(
            src_ref=buf.at[pl.ds(0, count)], dst_ref=buf.at[pl.ds(0, count)],
            send_sem=ssem.at[kind], recv_sem=rsem.at[kind],
            device_id=(me_r, me_c), device_id_type=MESH,
        )

    def arrived(buf, slot, kind):
        send(buf, slot, kind, (me_r, me_c)).wait_recv()

    mine = points[...]
    pts[me] = mine
    omg[me_r] = omega[...] * (0.5 / math.pi)
    pha[me_r] = phase[...].reshape(1, -1) * (0.5 / math.pi)
    wts[me_r] = weights[...].T.astype(jnp.bfloat16)
    high, mid, small = split(mine)
    own_sq = jnp.sum(mine * mine, 0, keepdims=True) * (-2.0 * LOG2E)
    ones = jnp.ones((8, B), jnp.float32)
    left = jnp.concatenate(
        (high, high, high, mid, mid, small, ones, rows_of(own_sq)), 0
    ).T.astype(jnp.bfloat16)

    pl.semaphore_wait(barrier, n - 1)

    def peer(k):
        return lax.rem(me_r + k + 1, R)

    def source(k):
        return lax.rem(me_r + R - 1 - k, R)

    def open_sends(k):
        to = (peer(k), me_c)
        send(omg, me_r, OMG, to).start()
        send(pha, me_r, PHA, to).start()
        send(wts, me_r, WTS, to).start()

    loop(R - 1, open_sends)

    def to_all(buf, kind):
        def one(k):
            j, to = other(k + 1)
            send(buf, me, kind, to).start()
        loop(n - 1, one)

    def from_all(buf, kind):
        many(buf, n - 1, kind).wait_recv()

    to_all(pts, PTS)

    for buf, kind in ((omg, OMG), (pha, PHA), (wts, WTS)):
        many(buf, R - 1, kind).wait_recv()

    width = omega.shape[1]
    group = 2 if width % 128 == 0 and R % 2 == 0 else 1

    def cat(buf, first, count):
        if count == 1:
            return buf[first]
        return jnp.concatenate([buf[first + i] for i in range(count)], 1)

    def features(g):
        o = cat(omg, g * group, group)
        p = cat(pha, g * group, group)
        right = right_stack(o, rows_of(p), jnp.zeros_like(o))
        turns = jnp.dot(left, right, preferred_element_type=jnp.float32)
        return nt(cat(wts, g * group, group), cosine(turns).astype(jnp.bfloat16))

    if R // group <= 32:
        prior = features(0)
        for g in range(1, R // group):
            prior = prior + features(g)
    else:
        prior = lax.fori_loop(
            0, R // group, lambda g, acc: acc + features(g), jnp.zeros((S, B), jnp.float32)
        )
    prior = scale * prior
    rhs = targets[...].reshape(1, -1) - prior - 0.5 * noise[...]

    low[me] = rhs.astype(jnp.bfloat16)

    def block_sends(buf, kind):
        loop(R - 1, lambda k: send(buf, me, kind, (peer(k), me_c)).start())

    def sibling(i):
        return lax.rem(me_c + i, C)

    def forward(buf, r, kind):
        for i in range(1, C):
            send(buf, me_c * R + r, kind + 2, (me_r, sibling(i))).start()

    block_sends(low, LOW)
    forward(low, me_r, LOW)

    eye = (
        lax.broadcasted_iota(jnp.int32, (S, 128), 0)
        == lax.broadcasted_iota(jnp.int32, (S, 128), 1)
    )

    def as_row(column):
        return jnp.sum(jnp.where(eye, column, 0.0), 0, keepdims=True)

    def as_column(row):
        return jnp.sum(jnp.where(eye, row, 0.0), 1, keepdims=True)

    rr_own = jnp.sum(rhs * rhs, 1, keepdims=True)
    st0[me] = as_row(rr_own)
    to_all(st0, ST0)

    from_all(pts, PTS)

    def kernel_chunk(g):
        b = cat(pts, g * C, C)
        sq = jnp.sum(b * b, 0, keepdims=True) * (-2.0 * LOG2E)
        right = right_stack(b * (4.0 * LOG2E), rows_of(sq), jnp.ones_like(b))
        power = jnp.dot(left, right, preferred_element_type=jnp.float32)
        kern[g] = jnp.exp2(power).astype(jnp.bfloat16)

    def relay(k):
        arrived(low, me_c * R + source(k), LOW)
        forward(low, source(k), LOW)
        kernel_chunk(k)

    loop(R - 1, relay)
    kernel_chunk(R - 1)

    def second_half(buf, kind):
        many(buf, R * (C - 1), kind + 2).wait_recv()

    second_half(low, LOW)

    def accumulate(block):
        if R <= 32:
            acc = nt(block(0), kern[0])
            for g in range(1, R):
                acc = acc + nt(block(g), kern[g])
            return acc
        return lax.fori_loop(
            0, R, lambda g, acc: acc + nt(block(g), kern[g]), jnp.zeros((S, B), jnp.float32)
        )

    part = accumulate(lambda g: cat(low, g * C, C))
    image = part + 0.25 * rhs
    share = jnp.sum(rhs * image, 1, keepdims=True)
    share = jnp.where(rr_own > 0.0, share / rr_own, 0.0)
    off = image - share * rhs
    img[me] = off.astype(jnp.bfloat16)
    block_sends(img, IMG)
    forward(img, me_r, IMG)
    st1[me] = jnp.concatenate(
        (
            as_row(share),
            as_row(jnp.sum(off * off, 1, keepdims=True)),
            as_row(jnp.sum(off * rhs, 1, keepdims=True)),
            jnp.zeros((1, 128), jnp.float32),
        ),
        0,
    )
    to_all(st1, ST1)
    from_all(st0, ST0)

    def relay_image(k):
        arrived(img, me_c * R + source(k), IMG)
        forward(img, source(k), IMG)

    loop(R - 1, relay_image)
    from_all(st1, ST1)
    norms = st0[:, 0, :]
    shares = st1[:, 0, :]
    squares = st1[:, 1, :]
    mixed = st1[:, 2, :]
    live = lax.broadcasted_iota(jnp.int32, (1, 128), 1) < S
    total = lambda x: jnp.sum(x, 0, keepdims=True)
    norm = total(norms)
    alpha = jnp.where(live, norm / total(shares * norms + mixed), 0.0)
    left_over = 1.0 - alpha * shares
    norm_next = total(
        left_over * left_over * norms
        + alpha * alpha * squares
        - 2.0 * alpha * left_over * mixed
    )
    beta = jnp.where(live, norm_next / norm, 0.0)
    coef[...] = beta + left_over
    alpha_c = as_column(alpha)
    beta_c = as_column(beta)
    residual = rhs - alpha_c * image
    direction = residual + beta_c * rhs
    posterior = prior + alpha_c * part

    second_half(img, IMG)

    def direction_block(j):
        c = as_column(coef[pl.ds(j, 1), :])
        return (c * low[j].astype(jnp.float32) - alpha_c * img[j].astype(jnp.float32)).astype(
            jnp.bfloat16
        )

    part = accumulate(
        lambda g: jnp.concatenate([direction_block(g * C + i) for i in range(C)], 1)
    )
    image = part + 0.25 * direction
    st2[me] = as_row(jnp.sum(direction * image, 1, keepdims=True))
    to_all(st2, ST2)

    for buf, kind in ((omg, OMG), (pha, PHA), (wts, WTS), (low, LOW), (img, IMG)):
        many(buf, R - 1, kind).wait_send()
    for buf, kind in ((low, LOWF), (img, IMGF)):
        many(buf, R * (C - 1), kind).wait_send()
    for buf, kind in ((pts, PTS), (st0, ST0), (st1, ST1)):
        many(buf, n - 1, kind).wait_send()

    from_all(st2, ST2)
    curve = total(st2[:, 0, :])
    alpha_c = as_column(jnp.where(live, norm_next / curve, 0.0))
    post_out[...] = posterior + alpha_c * part
    res_out[...] = residual - alpha_c * image
    many(st2, n - 1, ST2).wait_send()


def body(R, C, points, targets, noise, omega, phase, weights):
    n = R * C
    dim, B = points.shape
    width, S = weights.shape
    f32, bf16 = jnp.float32, jnp.bfloat16
    vmem = pl.BlockSpec(memory_space=pltpu.VMEM)
    return pl.pallas_call(
        functools.partial(kernel, R, C, math.sqrt(2.0 / (width * R))),
        out_shape=(
            jax.ShapeDtypeStruct(noise.shape, f32),
            jax.ShapeDtypeStruct(noise.shape, f32),
        ),
        in_specs=[vmem] * 6,
        out_specs=(vmem, vmem),
        scratch_shapes=[
            pltpu.VMEM((n, dim, B), f32),
            pltpu.VMEM((R, dim, width), f32),
            pltpu.VMEM((R, 1, width), f32),
            pltpu.VMEM((R, S, width), bf16),
            pltpu.VMEM((n, S, B), bf16),
            pltpu.VMEM((n, S, B), bf16),
            pltpu.VMEM((R, B, C * B), bf16),
            pltpu.VMEM((n, 1, 128), f32),
            pltpu.VMEM((n, 4, 128), f32),
            pltpu.VMEM((n, 1, 128), f32),
            pltpu.VMEM((n, 128), f32),
            pltpu.SemaphoreType.DMA((KINDS,)),
            pltpu.SemaphoreType.DMA((KINDS,)),
            pltpu.SemaphoreType.DMA((2, R)),
        ],
        compiler_params=pltpu.CompilerParams(collective_id=0, has_side_effects=True),
    )(points, targets, noise, omega, phase, weights)


def solution(mesh):
    return jax.shard_map(
        functools.partial(body, mesh.shape["rows"], mesh.shape["cols"]),
        mesh=mesh,
        in_specs=(
            P(None, ("cols", "rows")),
            P(("cols", "rows")),
            P(None, ("cols", "rows")),
            P(None, "rows"),
            P("rows"),
            P("rows", None),
        ),
        out_specs=(P(None, ("cols", "rows")), P(None, ("cols", "rows"))),
        check_vma=False,
    )
```

time: 326 us -> 50.5 us (0.15)
  blocking collectives: 311 us -> 0 us
  Pallas kernels: 0 us -> 46.1 us
  matrix products: 12.5 us -> 0 us
  local copies, waits for them, and re-layouts: 0.02 us -> 3.47 us
    all_gather x6 -> x0, blocking collectives: 237 us -> none  [the longest x2 81.4 us: body(): lax.all_gather(low, ('rows', 'cols'), axis=1, tiled=True)]
    psum x2 -> x0, blocking collectives: 73.7 us -> none  [body(): lax.psum((jnp.sum(direction * image, 1), jnp.sum(residual * image, 1), jn...]
    pallas_call x0 -> x1, Pallas kernels: none -> 46.1 us  [body(): pl.pallas_call(functools.partial(kernel, R, C, math.sqrt(2.0 / (width * R...]
    dot_general x5 -> x0, matrix products: 12.5 us -> none  [the longest x1 7.01 us: body(): lax.dot_general(wide_omega, points, (((0,), (0,)), ((), ())), precision=l...]
    unnamed x8 -> x5, local copies, waits for them, and re-layouts: 0.02 us -> 3.47 us
where the time goes in v1:
time: 50.5 us; the launch traced here: 50.2 us
  Pallas kernels  46.1 us (91%)
  local copies, waits for them, and re-layouts  3.47 us (7%)
  between operations  0.65 us (1%)
    pallas_call x1, Pallas kernels, body(): pl.pallas_call(functools.partial(kernel, R, C, math.sqrt(2.0 / (width * R...  46.1 us
    unnamed x5, local copies, waits for them, and re-layouts  3.47 us

profile of v1, /device:TPU:0, one launch (start us, length us, event | category | flops | bytes accessed | tf_op | source)
XLA Modules:
  0.0 50.2 jit_solution(4455414211982548643)
XLA Ops:
  0.6 1.5 %copy.8.weights = f32[128,64]{1,0:T(8,128)} copy(f32[128,64]{0,1:T(8,128)} %param.11) | data formatting | bytes 65536 | tf_op args[5]
  2.1 46.1 %shard_map.77 = (f32[64,128]{1,0:T(8,128)}, f32[64,128]{1,0:T(8,128)}) custom-call(f32[8,128]{1,0:T(8,128)} %points.1, f32[128]{0:T(128)} %targets.1, f32[64,128]{1,0:T(8,128)} %noise.1, f32[8,128]{1,0:T(8,128)} %omega.1, f32[128]{0:T(128)} %phase.1, f32[128,64]{1,0:T(8,128)} %copy.8.weights), custom_call_target="tpu_custom_call" | custom-call | tf_op jit(solution)/shard_map/pallas_call | solution.py:322
  48.2 0.0 copy-start
  48.2 1.4 %copy.11 = f32[64,128]{1,0:T(8,128)} copy(f32[64,128]{1,0:T(8,128)} %get-tuple-element.4) | data formatting | bytes 65536
  49.6 0.0 copy-done
  49.6 0.6 %copy.12 = f32[64,128]{1,0:T(8,128)} copy(f32[64,128]{1,0:T(8,128)S(1)} %copy-done) | data formatting | bytes 65536
Async XLA Ops:
  48.2 1.4 %copy-start = (f32[64,128]{1,0:T(8,128)S(1)}, f32[64,128]{1,0:T(8,128)}, u32[]{:S(2)}) copy-start(f32[64,128]{1,0:T(8,128)} %get-tuple-element.5) | copy-start | bytes 98308

commit v2 on v1

--- a/solution.py
+++ b/solution.py
@@ -19,8 +19,8 @@
     -25.96688461,
     6.527705963,
 )
-PTS, OMG, PHA, WTS, LOW, IMG, LOWF, IMGF, ST0, ST1, ST2 = range(11)
-KINDS = 11
+PTS, OMG, PHA, WTS, LOW, IMG, LAST = range(7)
+KINDS = 7
 
 
 def loop(count, body):
@@ -67,7 +67,7 @@
     R, C, scale,
     points, targets, noise, omega, phase, weights,
     post_out, res_out,
-    pts, omg, pha, wts, low, img, kern, st0, st1, st2, coef, ssem, rsem, slots,
+    pts, omg, pha, wts, low, img, kern, last, coef, ssem, rsem, slots,
 ):
     n = R * C
     me_r = lax.axis_index("rows")
@@ -87,29 +87,56 @@
 
     loop(n - 1, hello)
 
-    def send(buf, slot, kind, to):
+    A = 4 if R % 4 == 0 else 1
+    Q = R // A
+    plane = me_r // Q
+    place = lax.rem(me_r, Q)
+    NEAR, FAR, CORE = 0, 1, 2
+
+    def send(buf, slot, kind, way, to):
+        near = slots.at[kind, lax.rem(slot, R)]
         return pltpu.make_async_remote_copy(
             src_ref=buf.at[slot], dst_ref=buf.at[slot],
             send_sem=ssem.at[kind],
-            recv_sem=slots.at[kind - LOW, lax.rem(slot, R)] if kind in (LOW, IMG) else rsem.at[kind],
+            recv_sem=near if way == NEAR else rsem.at[kind, way],
             device_id=to, device_id_type=MESH,
         )
 
-    def many(buf, count, kind):
+    def many(buf, count, kind, way):
         return pltpu.make_async_remote_copy(
             src_ref=buf.at[pl.ds(0, count)], dst_ref=buf.at[pl.ds(0, count)],
-            send_sem=ssem.at[kind], recv_sem=rsem.at[kind],
+            send_sem=ssem.at[kind], recv_sem=rsem.at[kind, way],
             device_id=(me_r, me_c), device_id_type=MESH,
         )
 
-    def arrived(buf, slot, kind):
-        send(buf, slot, kind, (me_r, me_c)).wait_recv()
+    def to_planes(buf, kind, base):
+        def one(k):
+            to = lax.rem(plane + k + 1, A) * Q + place
+            send(buf, base + me_r, kind, NEAR, (to, me_c)).start()
+        loop(A - 1, one)
+
+    def to_places(buf, kind, base, r, way):
+        def one(k):
+            to = plane * Q + lax.rem(place + k + 1, Q)
+            send(buf, base + r, kind, way, (to, me_c)).start()
+        loop(Q - 1, one)
+
+    def to_cores(buf, kind, r):
+        for i in range(1, C):
+            to = (me_r, lax.rem(me_c + i, C))
+            send(buf, me_c * R + r, kind, CORE, to).start()
+
+    def from_plane(k):
+        return lax.rem(plane + A - 1 - k, A) * Q + place
+
+    def arrived(buf, kind, base, r):
+        send(buf, base + r, kind, NEAR, (me_r, me_c)).wait_recv()
 
     mine = points[...]
     pts[me] = mine
     omg[me_r] = omega[...] * (0.5 / math.pi)
     pha[me_r] = phase[...].reshape(1, -1) * (0.5 / math.pi)
-    wts[me_r] = weights[...].T.astype(jnp.bfloat16)
+    wts[me_r] = weights[...].astype(jnp.bfloat16)
     high, mid, small = split(mine)
     own_sq = jnp.sum(mine * mine, 0, keepdims=True) * (-2.0 * LOG2E)
     ones = jnp.ones((8, B), jnp.float32)
@@ -119,33 +146,32 @@
 
     pl.semaphore_wait(barrier, n - 1)
 
-    def peer(k):
-        return lax.rem(me_r + k + 1, R)
-
-    def source(k):
-        return lax.rem(me_r + R - 1 - k, R)
-
-    def open_sends(k):
-        to = (peer(k), me_c)
-        send(omg, me_r, OMG, to).start()
-        send(pha, me_r, PHA, to).start()
-        send(wts, me_r, WTS, to).start()
-
-    loop(R - 1, open_sends)
-
-    def to_all(buf, kind):
-        def one(k):
-            j, to = other(k + 1)
-            send(buf, me, kind, to).start()
-        loop(n - 1, one)
-
-    def from_all(buf, kind):
-        many(buf, n - 1, kind).wait_recv()
-
-    to_all(pts, PTS)
-
-    for buf, kind in ((omg, OMG), (pha, PHA), (wts, WTS)):
-        many(buf, R - 1, kind).wait_recv()
+    whole = me_c * R
+    rows_data = ((omg, OMG), (pha, PHA), (wts, WTS))
+    for buf, kind in rows_data:
+        to_planes(buf, kind, 0)
+    to_planes(pts, PTS, whole)
+    for buf, kind in rows_data:
+        to_places(buf, kind, 0, me_r, FAR)
+    to_places(pts, PTS, whole, me_r, NEAR)
+    to_cores(pts, PTS, me_r)
+
+    def relay_rows(k):
+        r = from_plane(k)
+        for buf, kind in rows_data:
+            arrived(buf, kind, 0, r)
+            to_places(buf, kind, 0, r, FAR)
+
+    def relay_points(k):
+        r = from_plane(k)
+        arrived(pts, PTS, whole, r)
+        to_places(pts, PTS, whole, r, NEAR)
+        to_cores(pts, PTS, r)
+
+    loop(A - 1, relay_rows)
+    loop(A - 1, relay_points)
+    for buf, kind in rows_data:
+        many(buf, R - A, kind, FAR).wait_recv()
 
     width = omega.shape[1]
     group = 2 if width % 128 == 0 and R % 2 == 0 else 1
@@ -175,18 +201,37 @@
 
     low[me] = rhs.astype(jnp.bfloat16)
 
-    def block_sends(buf, kind):
-        loop(R - 1, lambda k: send(buf, me, kind, (peer(k), me_c)).start())
-
-    def sibling(i):
-        return lax.rem(me_c + i, C)
-
-    def forward(buf, r, kind):
-        for i in range(1, C):
-            send(buf, me_c * R + r, kind + 2, (me_r, sibling(i))).start()
-
-    block_sends(low, LOW)
-    forward(low, me_r, LOW)
+    def far(k):
+        p = lax.rem(plane + k // (Q - 1), A) if Q > 1 else 0
+        return p * Q + lax.rem(place + 1 + lax.rem(k, max(Q - 1, 1)), Q)
+
+    def open_gather(buf, kind):
+        to_planes(buf, kind, whole)
+        to_places(buf, kind, whole, me_r, NEAR)
+        to_cores(buf, kind, me_r)
+
+    def relay_planes(buf, kind, work):
+        def one(k):
+            r = from_plane(k)
+            arrived(buf, kind, whole, r)
+            to_places(buf, kind, whole, r, NEAR)
+            to_cores(buf, kind, r)
+            work(k)
+        loop(A - 1, one)
+
+    def relay_places(buf, kind, work):
+        def one(k):
+            r = far(k)
+            arrived(buf, kind, whole, r)
+            to_cores(buf, kind, r)
+            work(k)
+        loop(A * (Q - 1), one)
+
+    def from_cores(buf, kind):
+        many(buf, R * (C - 1), kind, CORE).wait_recv()
+
+    open_gather(low, LOW)
+    relay_places(pts, PTS, lambda k: None)
 
     eye = (
         lax.broadcasted_iota(jnp.int32, (S, 128), 0)
@@ -200,10 +245,7 @@
         return jnp.sum(jnp.where(eye, row, 0.0), 1, keepdims=True)
 
     rr_own = jnp.sum(rhs * rhs, 1, keepdims=True)
-    st0[me] = as_row(rr_own)
-    to_all(st0, ST0)
-
-    from_all(pts, PTS)
+    from_cores(pts, PTS)
 
     def kernel_chunk(g):
         b = cat(pts, g * C, C)
@@ -212,18 +254,10 @@
         power = jnp.dot(left, right, preferred_element_type=jnp.float32)
         kern[g] = jnp.exp2(power).astype(jnp.bfloat16)
 
-    def relay(k):
-        arrived(low, me_c * R + source(k), LOW)
-        forward(low, source(k), LOW)
-        kernel_chunk(k)
-
-    loop(R - 1, relay)
+    relay_planes(low, LOW, kernel_chunk)
+    relay_places(low, LOW, lambda k: kernel_chunk(A - 1 + k))
     kernel_chunk(R - 1)
-
-    def second_half(buf, kind):
-        many(buf, R * (C - 1), kind + 2).wait_recv()
-
-    second_half(low, LOW)
+    from_cores(low, LOW)
 
     def accumulate(block):
         if R <= 32:
@@ -240,31 +274,27 @@
     share = jnp.sum(rhs * image, 1, keepdims=True)
     share = jnp.where(rr_own > 0.0, share / rr_own, 0.0)
     off = image - share * rhs
-    img[me] = off.astype(jnp.bfloat16)
-    block_sends(img, IMG)
-    forward(img, me_r, IMG)
-    st1[me] = jnp.concatenate(
-        (
-            as_row(share),
-            as_row(jnp.sum(off * off, 1, keepdims=True)),
-            as_row(jnp.sum(off * rhs, 1, keepdims=True)),
-            jnp.zeros((1, 128), jnp.float32),
-        ),
-        0,
-    )
-    to_all(st1, ST1)
-    from_all(st0, ST0)
-
-    def relay_image(k):
-        arrived(img, me_c * R + source(k), IMG)
-        forward(img, source(k), IMG)
-
-    loop(R - 1, relay_image)
-    from_all(st1, ST1)
-    norms = st0[:, 0, :]
-    shares = st1[:, 0, :]
-    squares = st1[:, 1, :]
-    mixed = st1[:, 2, :]
+    img[me, :S] = off.astype(jnp.bfloat16)
+    sums = (
+        as_row(rr_own),
+        as_row(share),
+        as_row(jnp.sum(off * off, 1, keepdims=True)),
+        as_row(jnp.sum(off * rhs, 1, keepdims=True)),
+    )
+    pieces = [split(row) for row in sums]
+    blank = jnp.zeros((4, 128), jnp.float32)
+    img[me, S:] = jnp.concatenate(
+        [p[i] for i in range(3) for p in pieces] + [blank], 0
+    ).astype(jnp.bfloat16)
+    open_gather(img, IMG)
+    relay_planes(img, IMG, lambda k: None)
+    relay_places(img, IMG, lambda k: None)
+    from_cores(img, IMG)
+
+    tail = img[:, S:, :].astype(jnp.float32)
+    norms, shares, squares, mixed = (
+        tail[:, i, :] + tail[:, 4 + i, :] + tail[:, 8 + i, :] for i in range(4)
+    )
     live = lax.broadcasted_iota(jnp.int32, (1, 128), 1) < S
     total = lambda x: jnp.sum(x, 0, keepdims=True)
     norm = total(norms)
@@ -283,11 +313,9 @@
     direction = residual + beta_c * rhs
     posterior = prior + alpha_c * part
 
-    second_half(img, IMG)
-
     def direction_block(j):
         c = as_column(coef[pl.ds(j, 1), :])
-        return (c * low[j].astype(jnp.float32) - alpha_c * img[j].astype(jnp.float32)).astype(
+        return (c * low[j].astype(jnp.float32) - alpha_c * img[j, :S].astype(jnp.float32)).astype(
             jnp.bfloat16
         )
 
@@ -295,28 +323,30 @@
         lambda g: jnp.concatenate([direction_block(g * C + i) for i in range(C)], 1)
     )
     image = part + 0.25 * direction
-    st2[me] = as_row(jnp.sum(direction * image, 1, keepdims=True))
-    to_all(st2, ST2)
-
-    for buf, kind in ((omg, OMG), (pha, PHA), (wts, WTS), (low, LOW), (img, IMG)):
-        many(buf, R - 1, kind).wait_send()
-    for buf, kind in ((low, LOWF), (img, IMGF)):
-        many(buf, R * (C - 1), kind).wait_send()
-    for buf, kind in ((pts, PTS), (st0, ST0), (st1, ST1)):
-        many(buf, n - 1, kind).wait_send()
-
-    from_all(st2, ST2)
-    curve = total(st2[:, 0, :])
+    last[me] = as_row(jnp.sum(direction * image, 1, keepdims=True))
+
+    def finish(k):
+        send(last, me, LAST, FAR, other(k + 1)[1]).start()
+
+    loop(n - 1, finish)
+    sent = (A - 1) + A * (Q - 1)
+    for buf, kind in rows_data:
+        many(buf, sent, kind, FAR).wait_send()
+    for buf, kind in ((pts, PTS), (low, LOW), (img, IMG)):
+        many(buf, sent + R * (C - 1), kind, FAR).wait_send()
+    many(last, n - 1, LAST, FAR).wait_recv()
+    curve = total(last[:, 0, :])
     alpha_c = as_column(jnp.where(live, norm_next / curve, 0.0))
     post_out[...] = posterior + alpha_c * part
     res_out[...] = residual - alpha_c * image
-    many(st2, n - 1, ST2).wait_send()
+    many(last, n - 1, LAST, FAR).wait_send()
 
 
 def body(R, C, points, targets, noise, omega, phase, weights):
     n = R * C
     dim, B = points.shape
-    width, S = weights.shape
+    weights = weights.T
+    S, width = weights.shape
     f32, bf16 = jnp.float32, jnp.bfloat16
     vmem = pl.BlockSpec(memory_space=pltpu.VMEM)
     return pl.pallas_call(
@@ -333,15 +363,13 @@
             pltpu.VMEM((R, 1, width), f32),
             pltpu.VMEM((R, S, width), bf16),
             pltpu.VMEM((n, S, B), bf16),
-            pltpu.VMEM((n, S, B), bf16),
+            pltpu.VMEM((n, S + 16, B), bf16),
             pltpu.VMEM((R, B, C * B), bf16),
-            pltpu.VMEM((n, 1, 128), f32),
-            pltpu.VMEM((n, 4, 128), f32),
             pltpu.VMEM((n, 1, 128), f32),
             pltpu.VMEM((n, 128), f32),
             pltpu.SemaphoreType.DMA((KINDS,)),
-            pltpu.SemaphoreType.DMA((KINDS,)),
-            pltpu.SemaphoreType.DMA((2, R)),
+            pltpu.SemaphoreType.DMA((KINDS, 3)),
+            pltpu.SemaphoreType.DMA((KINDS, R)),
         ],
         compiler_params=pltpu.CompilerParams(collective_id=0, has_side_effects=True),
     )(points, targets, noise, omega, phase, weights)

time: 50.5 us -> 44.8 us (0.89)
  Pallas kernels: 46.1 us -> 41.9 us
  local copies, waits for them, and re-layouts: 3.47 us -> 2 us
    pallas_call x1, Pallas kernels: 46.1 us -> 41.9 us  [body(): pl.pallas_call(functools.partial(kernel, R, C, math.sqrt(2.0 / (width * R...]
    unnamed x5 -> x4, local copies, waits for them, and re-layouts: 3.47 us -> 2 us
where the time goes in v2:
time: 44.8 us; the launch traced here: 44.6 us
  Pallas kernels  41.9 us (94%)
  local copies, waits for them, and re-layouts  2 us (4%)
  between operations  0.65 us (1%)
    pallas_call x1, Pallas kernels, body(): pl.pallas_call(functools.partial(kernel, R, C, math.sqrt(2.0 / (width * R...  41.9 us
    unnamed x4, local copies, waits for them, and re-layouts  2 us

profile of v2, /device:TPU:0, one launch (start us, length us, event | category | flops | bytes accessed | tf_op | source)
XLA Modules:
  0.0 44.6 jit_solution(5777532179740197178)
XLA Ops:
  0.6 41.9 %shard_map.77 = (f32[64,128]{1,0:T(8,128)}, f32[64,128]{1,0:T(8,128)}) custom-call(f32[8,128]{1,0:T(8,128)} %points.1, f32[128]{0:T(128)} %targets.1, f32[64,128]{1,0:T(8,128)} %noise.1, f32[8,128]{1,0:T(8,128)} %omega.1, f32[128]{0:T(128)} %phase.1, f32[64,128]{1,0:T(8,128)} %bitcast.1), custom_call_target="tpu_custom_call" | custom-call | tf_op jit(solution)/shard_map/pallas_call | solution.py:352
  42.6 0.0 copy-start
  42.6 1.4 %copy.10 = f32[64,128]{1,0:T(8,128)} copy(f32[64,128]{1,0:T(8,128)} %get-tuple-element.4) | data formatting | bytes 65536
  44.0 0.0 copy-done
  44.0 0.6 %copy.11 = f32[64,128]{1,0:T(8,128)} copy(f32[64,128]{1,0:T(8,128)S(1)} %copy-done) | data formatting | bytes 65536
Async XLA Ops:
  42.6 1.4 %copy-start = (f32[64,128]{1,0:T(8,128)S(1)}, f32[64,128]{1,0:T(8,128)}, u32[]{:S(2)}) copy-start(f32[64,128]{1,0:T(8,128)} %get-tuple-element.5) | copy-start | bytes 98308

commit v3 on v2

--- a/solution.py
+++ b/solution.py
@@ -82,16 +82,18 @@
         j = lax.rem(me + k, n)
         return j, (lax.rem(j, R), j // R)
 
-    def hello(k):
-        pl.semaphore_signal(barrier, inc=1, device_id=other(k + 1)[1], device_id_type=MESH)
-
-    loop(n - 1, hello)
-
     A = 4 if R % 4 == 0 else 1
     Q = R // A
     plane = me_r // Q
     place = lax.rem(me_r, Q)
     NEAR, FAR, CORE = 0, 1, 2
+
+    def hello(r, c):
+        pl.semaphore_signal(barrier, inc=1, device_id=(r, c), device_id_type=MESH)
+
+    loop(A - 1, lambda k: hello(lax.rem(plane + k + 1, A) * Q + place, me_c))
+    loop(Q - 1, lambda k: hello(plane * Q + lax.rem(place + k + 1, Q), me_c))
+    loop(C - 1, lambda k: hello(me_r, lax.rem(me_c + k + 1, C)))
 
     def send(buf, slot, kind, way, to):
         near = slots.at[kind, lax.rem(slot, R)]
@@ -144,7 +146,7 @@
         (high, high, high, mid, mid, small, ones, rows_of(own_sq)), 0
     ).T.astype(jnp.bfloat16)
 
-    pl.semaphore_wait(barrier, n - 1)
+    pl.semaphore_wait(barrier, A + Q + C - 3)
 
     whole = me_c * R
     rows_data = ((omg, OMG), (pha, PHA), (wts, WTS))
@@ -219,19 +221,20 @@
             work(k)
         loop(A - 1, one)
 
-    def relay_places(buf, kind, work):
+    def relay_places(buf, kind, work, first=0, last=A * (Q - 1)):
         def one(k):
-            r = far(k)
+            r = far(first + k)
             arrived(buf, kind, whole, r)
             to_cores(buf, kind, r)
             work(k)
-        loop(A * (Q - 1), one)
+        loop(last - first, one)
 
     def from_cores(buf, kind):
         many(buf, R * (C - 1), kind, CORE).wait_recv()
 
     open_gather(low, LOW)
-    relay_places(pts, PTS, lambda k: None)
+    idle = lambda k: None
+    relay_places(pts, PTS, idle)
 
     eye = (
         lax.broadcasted_iota(jnp.int32, (S, 128), 0)
@@ -254,9 +257,16 @@
         power = jnp.dot(left, right, preferred_element_type=jnp.float32)
         kern[g] = jnp.exp2(power).astype(jnp.bfloat16)
 
-    relay_planes(low, LOW, kernel_chunk)
-    relay_places(low, LOW, lambda k: kernel_chunk(A - 1 + k))
-    kernel_chunk(R - 1)
+    head = R // 4
+    each = R // 8
+    done = head + (A - 1) * each
+    loop(head, kernel_chunk)
+    relay_planes(low, LOW, lambda k: loop(each, lambda i: kernel_chunk(head + k * each + i)))
+    steps = A * (Q - 1)
+    paired = min(R - done, steps - (Q - 1))
+    relay_places(low, LOW, idle, 0, steps - paired)
+    relay_places(low, LOW, lambda k: kernel_chunk(done + k), steps - paired, steps)
+    loop(R - done - paired, lambda k: kernel_chunk(done + paired + k))
     from_cores(low, LOW)
 
     def accumulate(block):
@@ -287,8 +297,8 @@
         [p[i] for i in range(3) for p in pieces] + [blank], 0
     ).astype(jnp.bfloat16)
     open_gather(img, IMG)
-    relay_planes(img, IMG, lambda k: None)
-    relay_places(img, IMG, lambda k: None)
+    relay_planes(img, IMG, idle)
+    relay_places(img, IMG, idle)
     from_cores(img, IMG)
 
     tail = img[:, S:, :].astype(jnp.float32)

time: 44.8 us -> 43.8 us (0.978)
  Pallas kernels: 41.9 us -> 40.9 us
    pallas_call x1, Pallas kernels: 41.9 us -> 40.9 us  [body(): pl.pallas_call(functools.partial(kernel, R, C, math.sqrt(2.0 / (width * R...]
where the time goes in v3:
time: 43.8 us; the launch traced here: 43.6 us
  Pallas kernels  40.9 us (93%)
  local copies, waits for them, and re-layouts  2 us (5%)
  between operations  0.65 us (1%)
    pallas_call x1, Pallas kernels, body(): pl.pallas_call(functools.partial(kernel, R, C, math.sqrt(2.0 / (width * R...  40.9 us
    unnamed x4, local copies, waits for them, and re-layouts  2 us

profile of v3, /device:TPU:0, one launch (start us, length us, event | category | flops | bytes accessed | tf_op | source)
XLA Modules:
  0.0 43.6 jit_solution(13181844134187928736)
XLA Ops:
  0.6 40.9 %shard_map.77 = (f32[64,128]{1,0:T(8,128)}, f32[64,128]{1,0:T(8,128)}) custom-call(f32[8,128]{1,0:T(8,128)} %points.1, f32[128]{0:T(128)} %targets.1, f32[64,128]{1,0:T(8,128)} %noise.1, f32[8,128]{1,0:T(8,128)} %omega.1, f32[128]{0:T(128)} %phase.1, f32[64,128]{1,0:T(8,128)} %bitcast.1), custom_call_target="tpu_custom_call" | custom-call | tf_op jit(solution)/shard_map/pallas_call | solution.py:362
  41.6 0.0 copy-start
  41.6 1.4 %copy.10 = f32[64,128]{1,0:T(8,128)} copy(f32[64,128]{1,0:T(8,128)} %get-tuple-element.4) | data formatting | bytes 65536
  42.9 0.0 copy-done
  42.9 0.6 %copy.11 = f32[64,128]{1,0:T(8,128)} copy(f32[64,128]{1,0:T(8,128)S(1)} %copy-done) | data formatting | bytes 65536
Async XLA Ops:
  41.6 1.4 %copy-start = (f32[64,128]{1,0:T(8,128)S(1)}, f32[64,128]{1,0:T(8,128)}, u32[]{:S(2)}) copy-start(f32[64,128]{1,0:T(8,128)} %get-tuple-element.5) | copy-start | bytes 98308
